TPU v7x, 32 devices: a whole 2x2x4 slice. The times are simulated.
32 devices in a mesh: samp: 16 (over z, y, x), tgt: 2 (over core).
Axes of the slice: x: 2, y: 2, z: 4, core: 2. Of those that a mesh axis runs over, the one named last changes fastest.
Arguments:
- samples: bfloat16 [3072, 128], P('samp'), may hold values from -6 to 6
- omega: bfloat16 [128, 4096], replicated, may hold values from -0.5 to 0.5
- phase: float32 [4096], replicated, may hold values from -3.140625 to 3.140625
- right_side: float32 [4096, 512], P('samp', 'tgt'), may hold values from -6 to 6
Outputs:
- weights: float32 [4096, 512], P('samp', 'tgt')
All inputs are finite; a program needn't handle non-finite values.
Results may differ from a plain program's by a relative error of at most 0.011.
The roundings to bfloat16 on the way count: a program that leaves them out, or rounds other values in their place, can miss the bound.
Values may be sent and summed in bfloat16 or wider, within the bound.
A program may use at most 128 MiB of HBM per device.

v0:
```python
import math
import jax
import jax.numpy as jnp
from jax import lax
from jax.sharding import PartitionSpec as P

ITERS = 2
ridge = 1.0


def precise_dot(left_matrix, right_matrix):
    return jnp.dot(left_matrix, right_matrix, precision=lax.Precision.HIGHEST)


def spd_solve(gram_matrix, rhs_matrix):
    factor = jnp.linalg.cholesky(gram_matrix)
    return jax.scipy.linalg.cho_solve((factor, True), rhs_matrix)


def cosine_block(samples, omega, phase, first_row, row_count):
    omega_cols = lax.dynamic_slice_in_dim(omega, first_row, row_count, 1)
    phase_cols = lax.dynamic_slice_in_dim(phase, first_row, row_count, 0)
    preact = jnp.dot(samples, omega_cols, preferred_element_type=jnp.float32) + phase_cols
    return jnp.cos(preact).astype(jnp.bfloat16)


def full_gram(stacked):
    summed = lax.psum(stacked, "samp")
    return lax.all_gather(summed, "tgt", axis=2, tiled=True)


def body(samples, omega, phase, right_side):
    feat_rows, col_count = right_side.shape
    samp_count = lax.axis_size("samp")
    feat_total = omega.shape[1]
    sample_total = samples.shape[0] * samp_count
    col_offset = lax.axis_index("tgt") * col_count
    store_block = math.gcd(feat_total, 512)
    stored = jnp.concatenate(
        [
            cosine_block(samples, omega, phase, index_block * store_block, store_block)
            for index_block in range(feat_total // store_block)
        ],
        axis=1,
    )

    def columns(first_row, row_count):
        return lax.dynamic_slice_in_dim(stored, first_row, row_count, 1)

    resid_all = lax.all_gather(right_side, "tgt", axis=1, tiled=True)
    direction_all = resid_all
    weight_own = jnp.zeros_like(right_side)
    gram_rr = full_gram(precise_dot(resid_all.T, right_side)[None])[0]
    for iteration in range(ITERS):
        direction_own = lax.dynamic_slice_in_dim(direction_all, col_offset, col_count, 1)
        initial = jnp.zeros((samples.shape[0], col_count), jnp.float32)
        shard_piece = lax.all_gather(direction_own.astype(jnp.bfloat16), "samp", axis=0, tiled=True)
        piece_rows = shard_piece.shape[0]
        block_size = math.gcd(piece_rows, 512)

        def project_one_block(index_block, acc_value):
            begin_row = index_block * block_size
            sub_piece = lax.dynamic_slice_in_dim(shard_piece, begin_row, block_size, 0)
            return acc_value + jnp.dot(
                columns(begin_row, block_size), sub_piece, preferred_element_type=jnp.float32
            )

        projected = lax.fori_loop(0, piece_rows // block_size, project_one_block, initial)
        proj_bf = projected.astype(jnp.bfloat16)
        transpose_row_count = feat_rows * lax.axis_size("samp")
        transpose_block_size = math.gcd(transpose_row_count, 512)

        def transpose_one_block(index_block, result):
            begin_row = index_block * transpose_block_size
            feats_block = columns(begin_row, transpose_block_size)
            block_term = lax.dot_general(
                feats_block, proj_bf, (((0,), (0,)), ((), ())), preferred_element_type=jnp.float32
            )
            return lax.dynamic_update_slice_in_dim(result, block_term, begin_row, 0)

        zero_rows = jnp.zeros((transpose_row_count, col_count), jnp.float32)
        summed_image = lax.psum_scatter(
            lax.fori_loop(
                0, transpose_row_count // transpose_block_size, transpose_one_block, zero_rows
            ),
            "samp",
            scatter_dimension=0,
            tiled=True,
        )
        image_own = summed_image / sample_total + ridge * direction_own
        image_all = lax.all_gather(image_own, "tgt", axis=1, tiled=True)
        gram_pq = full_gram(precise_dot(direction_all.T, image_own)[None])[0]
        alpha_coef = spd_solve(gram_pq, gram_rr)
        alpha_own = lax.dynamic_slice_in_dim(alpha_coef, col_offset, col_count, 1)
        weight_own = weight_own + precise_dot(direction_all, alpha_own)
        if iteration + 1 < ITERS:
            resid_all = resid_all - precise_dot(image_all, alpha_coef)
            resid_now = lax.dynamic_slice_in_dim(resid_all, col_offset, col_count, 1)
            gram_new = full_gram(precise_dot(resid_all.T, resid_now)[None])[0]
            beta_coef = spd_solve(gram_rr, gram_new)
            direction_all = resid_all + precise_dot(direction_all, beta_coef)
            gram_rr = gram_new
    return weight_own


def solution(mesh):
    placed = (P("samp", None), P(), P(), P("samp", "tgt"))
    return jax.shard_map(
        body, mesh=mesh, in_specs=placed, out_specs=P("samp", "tgt"), check_vma=False
    )
```

profile of v0, /device:TPU:0, one launch (start us, length us, event | category | flops | bytes accessed | tf_op | source)
XLA Modules:
  0.0 1215.1 jit_solution(10789328759363507932)
XLA Ops:
  6.5 2.6 all_gather.24
  22.8 50.4 %all-gather.7.cloned.1.call-done = bf16[4096,256]{1,0:T(8,128)(2,1)} async-done(((bf16[256,256]{1,0:T(8,128)(2,1)}), bf16[4096,256]{1,0:T(8,128)(2,1)}) %all-gather.7.cloned.1.call-update) | async-done | bytes 2097168 | tf_op jit(solution)/shard_map/all_gather | solution.py:57
  73.3 9.8 while.62
  85.3 8.6 while.60
  96.3 91.8 %reduce-scatter.3.cloned.1.call-done = f32[256,256]{1,0:T(8,128)} async-done(((f32[4096,256]{1,0:T(8,128)}), f32[256,256]{1,0:T(8,128)}) %reduce-scatter.3.cloned.1.call-update) | async-done | bytes 262160 | tf_op jit(solution)/shard_map/reduce_scatter | solution.py:82
  190.6 114.9 %all-reduce.10.cloned.1.call-done = (f32[1,512,256]{1,2,0:T(8,128)}, f32[1,512,256]{1,2,0:T(8,128)}) async-done(((f32[1,512,256]{1,2,0:T(8,128)}, f32[1,512,256]{1,2,0:T(8,128)}), (f32[1,512,256]{1,2,0:T(8,128)}, f32[1,512,256]{1,2,0:T(8,128)})) %all-reduce.10.cloned.1.call-update) | async-done | bytes 1048592 | tf_op jit(solution)/shard_map/psum | solution.py:28
  307.9 7.1 all-gather.9.cloned.1.call-done
  315.0 2.6 copy.5
  320.1 11.7 cholesky.374
  332.0 9.8 custom-call.35
  344.3 11.7 cholesky.393
  356.1 10.0 custom-call.36
  367.6 11.7 cholesky.414
  380.0 9.8 custom-call.37
  391.3 11.7 cholesky.431
  408.6 12.0 while.64
  420.6 39.3 %custom-call.38 = f32[4,128,128]{1,2,0:T(8,128)S(1)} custom-call(f32[4,128,128]{2,1,0:T(8,128)S(1)} %get-tuple-element.377), custom_call_target="InvertDiagBlocksLowerTriangular" | custom-call | tf_op jit(solution)/shard_map/jit(_cho_solve)/triangular_solve | solution.py:17
  460.0 2.7 copy.7
  475.0 11.7 cholesky.446
  487.5 10.8 custom-call.39
  502.1 12.5 %cholesky.465 = f32[128,128]{1,0:T(8,128)S(1)} custom-call(f32[128,128]{1,0:T(8,128)} %cholesky.603), custom_call_target="Cholesky" | custom-call | tf_op jit(solution)/shard_map/jit(cholesky)/cholesky | solution.py:16
  515.3 10.6 custom-call.40
  529.1 12.5 %cholesky.486 = f32[128,128]{1,0:T(8,128)} custom-call(f32[128,128]{1,0:T(8,128)S(1)} %cholesky.608), custom_call_target="Cholesky" | custom-call | tf_op jit(solution)/shard_map/jit(cholesky)/cholesky | solution.py:16
  543.1 10.4 custom-call.41
  555.9 12.3 %cholesky.503 = f32[128,128]{1,0:T(8,128)} custom-call(f32[128,128]{1,0:T(8,128)S(1)} %convolution_subtract_fusion.26), custom_call_target="Cholesky" | custom-call | tf_op jit(solution)/shard_map/jit(cholesky)/cholesky | solution.py:16
  578.3 105.3 %all-reduce.6.cloned.1.call-done = f32[1,512,256]{2,1,0:T(8,128)} async-done(((f32[1,512,256]{2,1,0:T(8,128)}), f32[1,512,256]{2,1,0:T(8,128)}) %all-reduce.6.cloned.1.call-update) | async-done | bytes 524304 | tf_op jit(solution)/shard_map/psum | solution.py:28
  684.4 14.8 %while.65 = (s32[]{:T(128)}, f32[512,512]{1,0:T(8,128)}, s32[4,2]{0,1:T(2,128)S(1)}, f32[4,128,128]{2,1,0:T(8,128)}, s32[]{:T(128)}) while((s32[]{:T(128)}, f32[512,512]{1,0:T(8,128)}, s32[4,2]{0,1:T(2,128)S(1)}, f32[4,128,128]{2,1,0:T(8,128)}, s32[]{:T(128)}) %tuple.227), condition=%wide.while_cond.clone, body=%wide.while_body.clone.sunk | while | flops 2 | bytes 132705 | solution.py:17
  685.5 2.9 bitcast_dynamic-update-slice_fusion.7
  689.1 3.0 bitcast_dynamic-update-slice_fusion.7
  692.7 2.9 bitcast_dynamic-update-slice_fusion.7
  696.3 2.9 bitcast_dynamic-update-slice_fusion.7
  699.2 40.8 %custom-call.42 = f32[4,128,128]{1,2,0:T(8,128)} custom-call(f32[4,128,128]{2,1,0:T(8,128)} %get-tuple-element.378), custom_call_target="InvertDiagBlocksLowerTriangular" | custom-call | tf_op jit(solution)/shard_map/jit(_cho_solve)/triangular_solve | solution.py:17
  752.9 59.5 %all-gather.15.cloned.1.call-done = bf16[4096,256]{1,0:T(8,128)(2,1)} async-done(((bf16[256,256]{1,0:T(8,128)(2,1)}), bf16[4096,256]{1,0:T(8,128)(2,1)}) %all-gather.15.cloned.1.call-update) | async-done | bytes 2097168 | tf_op jit(solution)/shard_map/all_gather | solution.py:57
  812.4 9.8 while.63
  824.4 8.6 while.61
  833.1 94.1 %reduce-scatter.5.cloned.1.call-done = f32[256,256]{1,0:T(8,128)} async-done(((f32[4096,256]{1,0:T(8,128)}), f32[256,256]{1,0:T(8,128)}) %reduce-scatter.5.cloned.1.call-update) | async-done | bytes 262160 | tf_op jit(solution)/shard_map/reduce_scatter | solution.py:82
  929.9 111.0 %all-reduce.8.cloned.1.call-done = f32[1,512,256]{1,2,0:T(8,128)} async-done(((f32[1,512,256]{1,2,0:T(8,128)}), f32[1,512,256]{1,2,0:T(8,128)}) %all-reduce.8.cloned.1.call-update) | async-done | bytes 524304 | tf_op jit(solution)/shard_map/psum | solution.py:28
  1042.0 8.5 all-gather.17.cloned.1.call-done
  1050.5 2.6 copy.10
  1055.6 11.7 cholesky.518
  1067.5 9.8 custom-call.43
  1079.8 11.7 cholesky.537
  1092.9 10.0 custom-call.44
  1104.4 11.7 cholesky.558
  1116.8 9.8 custom-call.45
  1128.1 11.7 cholesky.575
  1144.4 11.5 while.66
  1155.9 39.3 %custom-call.46 = f32[4,128,128]{1,2,0:T(8,128)S(1)} custom-call(f32[4,128,128]{2,1,0:T(8,128)S(1)} %get-tuple-element.379), custom_call_target="InvertDiagBlocksLowerTriangular" | custom-call | tf_op jit(solution)/shard_map/jit(_cho_solve)/triangular_solve | solution.py:17
  (276 shorter events, 173.6 us)
Async XLA Ops:
  6.5 4.2 copy-start
  6.5 6.5 copy-start.26
  6.5 66.7 %all-gather.7.cloned.1.call-start = ((), (), s32[]{:S(2)}) async-start(), calls=%async_computation.2 | async-start | bytes 2228224 | tf_op jit(solution)/shard_map/all_gather | solution.py:57
  9.9 178.2 %reduce-scatter.3.cloned.1.call-start = ((), (), s32[]{:S(2)}) async-start(), calls=%async_computation.3 | async-start | bytes 4456448 | tf_op jit(solution)/shard_map/reduce_scatter | solution.py:82
  93.9 0.9 copy-start.19
  93.9 211.5 %all-reduce.10.cloned.1.call-start = ((), (), s32[]{:S(2)}) async-start(), calls=%async_computation.12 | async-start | bytes 2097152 | tf_op jit(solution)/shard_map/psum | solution.py:28
  190.5 124.4 %all-gather.9.cloned.1.call-start = ((), (), s32[]{:S(2)}) async-start(), calls=%async_computation.4 | async-start | bytes 1572864 | tf_op jit(solution)/shard_map/all_gather | solution.py:29
  305.5 154.5 %all-gather.11.cloned.1.call-start = ((), (), s32[]{:S(2)}) async-start(), calls=%async_computation.5 | async-start | bytes 1572864 | tf_op jit(solution)/shard_map/all_gather | solution.py:29
  307.8 375.8 %all-reduce.6.cloned.1.call-start = ((), (), s32[]{:S(2)}) async-start(), calls=%async_computation.6 | async-start | bytes 1048576 | tf_op jit(solution)/shard_map/psum | solution.py:28
  315.0 2.7 copy-start.9
  319.1 1.0 copy-start.15
  459.9 7.9 copy-start.20
  460.0 2.7 copy-start.1
  462.6 2.3 copy-start.7
  468.2 3.4 copy-start.21
  471.2 1.6 copy-start.2
  471.7 2.2 copy-start.10
  472.0 2.0 copy-start.12
  474.1 1.0 copy-start.16
  500.8 0.7 copy-start.23
  528.4 0.7 copy-start.24
  568.2 7.6 copy-start.25
  570.6 0.8 copy-start.4
  573.2 166.8 %all-gather.13.cloned.1.call-start = ((), (), s32[]{:S(2)}) async-start(), calls=%async_computation.7 | async-start | bytes 1572864 | tf_op jit(solution)/shard_map/all_gather | solution.py:29
  683.6 128.7 %all-gather.15.cloned.1.call-start = ((), (), s32[]{:S(2)}) async-start(), calls=%async_computation.8 | async-start | bytes 2228224 | tf_op jit(solution)/shard_map/all_gather | solution.py:57
  699.2 44.9 %copy-start.6 = (f32[512,512]{1,0:T(8,128)S(1)}, f32[512,512]{1,0:T(8,128)}, u32[]{:S(2)}) copy-start(f32[512,512]{1,0:T(8,128)} %get-tuple-element.842) | copy-start | bytes 3145732
  740.0 5.5 copy-start.22
  749.6 1.4 copy-start.5
  752.8 174.4 %reduce-scatter.5.cloned.1.call-start = ((), (), s32[]{:S(2)}) async-start(), calls=%async_computation.9 | async-start | bytes 4456448 | tf_op jit(solution)/shard_map/reduce_scatter | solution.py:82
  833.0 207.9 %copy-start.3 = (f32[128,512]{1,0:T(8,128)S(1)}, f32[128,512]{1,0:T(8,128)}, u32[]{:S(2)}) copy-start(f32[128,512]{1,0:T(8,128)} %copy-done.2) | copy-start | bytes 786436
  833.0 207.9 %copy-start.13 = (f32[128,512]{1,0:T(8,128)S(1)}, f32[128,512]{1,0:T(8,128)}, u32[]{:S(2)}) copy-start(f32[128,512]{1,0:T(8,128)} %copy-done.12) | copy-start | bytes 786436
  833.0 207.9 %copy-start.18 = (f32[128,512]{1,0:T(8,128)S(1)}, f32[128,512]{1,0:T(8,128)}, u32[]{:S(2)}) copy-start(f32[128,512]{1,0:T(8,128)} %fusion.170) | copy-start | bytes 786436
  833.0 207.9 %all-reduce.8.cloned.1.call-start = ((), (), s32[]{:S(2)}) async-start(), calls=%async_computation.10 | async-start | bytes 1048576 | tf_op jit(solution)/shard_map/psum | solution.py:28
  929.7 120.8 %all-gather.17.cloned.1.call-start = ((), (), s32[]{:S(2)}) async-start(), calls=%async_computation.11 | async-start | bytes 1572864 | tf_op jit(solution)/shard_map/all_gather | solution.py:29
  1050.5 2.7 copy-start.11
  1054.6 1.0 copy-start.14
  1155.9 42.5 %copy-start.8 = (f32[512,512]{1,0:T(8,128)S(1)}, f32[512,512]{1,0:T(8,128)}, u32[]{:S(2)}) copy-start(f32[512,512]{1,0:T(8,128)} %get-tuple-element.844) | copy-start | bytes 3145732
  1204.9 1.4 copy-start.17
Sparse Core Ops, SparseCore 0:
  10.1 63.1 all-gather.6
  94.0 94.0 reduce-scatter.2
  193.4 111.9 all-reduce.9
  306.8 8.0 all-gather.8
  316.4 10.1 all-gather.10
  573.3 110.2 all-reduce.5
  685.2 8.0 all-gather.12
  752.9 59.3 all-gather.14
  833.1 94.0 reduce-scatter.4
  932.2 108.6 all-reduce.7
  1042.4 8.0 all-gather.16
where the time goes:
time: 1230 us; the launch traced here: 1220 us
  waiting for transfers between devices  643 us (52%)
  other arithmetic  372 us (30%)
  matrix products  111 us (9%)
  local copies, waits for them, and re-layouts  60.6 us (5%)
  between operations  22.3 us (2%)
    psum x3, waiting for transfers between devices, full_gram(): summed = lax.psum(stacked, 'samp')  331 us
    another operation x43, other arithmetic, spd_solve(): factor = jnp.linalg.cholesky(gram_matrix)  243 us
    reduce_scatter x2, waiting for transfers between devices, body(): lax.psum_scatter(lax.fori_loop(0, transpose_row_count // transpose_block_...  186 us
    another operation x8, other arithmetic, spd_solve(): return jax.scipy.linalg.cho_solve((factor, True), rhs_matrix)  124 us
    all_gather x2, waiting for transfers between devices, body(): lax.all_gather(direction_own.astype(jnp.bfloat16), 'samp', axis=0, tiled=...  110 us
    another operation x40, local copies, waits for them, and re-layouts, spd_solve(): return jax.scipy.linalg.cho_solve((factor, True), rhs_matrix)  38.5 us
    another operation x42, matrix products, spd_solve(): return jax.scipy.linalg.cho_solve((factor, True), rhs_matrix)  31.8 us
  transfers between devices with their start and end apart: 11, of which 9 were waited for; matrix products, arithmetic and copies ran while one was open for 18% of the time, Pallas kernels for 0%

commit v1 on v0

--- a/solution.py
+++ b/solution.py
@@ -6,6 +6,25 @@
 
 ITERS = 2
 ridge = 1.0
+
+
+def joined_along(pieces, dim):
+    pieces = jnp.moveaxis(pieces, 0, dim)
+    lengths = pieces.shape
+    return pieces.reshape(*lengths[:dim], lengths[dim] * lengths[dim + 1], *lengths[dim + 2 :])
+
+
+def doubled(array, axis):
+    size, index = (lax.axis_size(axis), lax.axis_index(axis))
+    blocks, bit = (array[None], 1)
+    while bit < size:
+        received = lax.ppermute(blocks, axis, [(i, i ^ bit) for i in range(size)])
+        low = index & bit == 0
+        blocks = jnp.concatenate(
+            [jnp.where(low, blocks, received), jnp.where(low, received, blocks)]
+        )
+        bit *= 2
+    return blocks
 
 
 def precise_dot(left_matrix, right_matrix):
@@ -54,7 +73,8 @@
     for iteration in range(ITERS):
         direction_own = lax.dynamic_slice_in_dim(direction_all, col_offset, col_count, 1)
         initial = jnp.zeros((samples.shape[0], col_count), jnp.float32)
-        shard_piece = lax.all_gather(direction_own.astype(jnp.bfloat16), "samp", axis=0, tiled=True)
+        shard = direction_own.astype(jnp.bfloat16)
+        shard_piece = joined_along(doubled(shard, "samp"), 0)
         piece_rows = shard_piece.shape[0]
         block_size = math.gcd(piece_rows, 512)
 

time: 1230 us -> 1250 us (1.016)
  starting transfers between devices: 0.93 us -> 15.6 us
    all_gather x2 -> x0, waiting for transfers between devices: 110 us -> none  [body(): lax.all_gather(direction_own.astype(jnp.bfloat16), 'samp', axis=0, tiled=...]
    ppermute x0 -> x8, waiting for transfers between devices: none -> 104 us  [doubled(): received = lax.ppermute(blocks, axis, [(i, i ^ bit) for i in range(size)])]
    ppermute x0 -> x8, starting transfers between devices: none -> 15.1 us  [doubled(): received = lax.ppermute(blocks, axis, [(i, i ^ bit) for i in range(size)])]
  transfers between devices with their start and end apart: 11 -> 17, of which waited for: 9 -> 15; matrix products, arithmetic and copies ran while one was open for 18% -> 18% of each run, Pallas kernels for 0% -> 0%
where the time goes in v1:
time: 1250 us; the launch traced here: 1240 us
  waiting for transfers between devices  640 us (51%)
  other arithmetic  382 us (31%)
  matrix products  117 us (9%)
  local copies, waits for them, and re-layouts  58.9 us (5%)
  between operations  22.5 us (2%)
  starting transfers between devices  15.6 us (1%)
    psum x3, waiting for transfers between devices, full_gram(): summed = lax.psum(stacked, 'samp')  331 us
    another operation x43, other arithmetic, spd_solve(): factor = jnp.linalg.cholesky(gram_matrix)  243 us
    reduce_scatter x2, waiting for transfers between devices, body(): lax.psum_scatter(lax.fori_loop(0, transpose_row_count // transpose_block_...  188 us
    another operation x8, other arithmetic, spd_solve(): return jax.scipy.linalg.cho_solve((factor, True), rhs_matrix)  124 us
    ppermute x8, waiting for transfers between devices, doubled(): received = lax.ppermute(blocks, axis, [(i, i ^ bit) for i in range(size)])  104 us
    another operation x40, local copies, waits for them, and re-layouts, spd_solve(): return jax.scipy.linalg.cho_solve((factor, True), rhs_matrix)  37.7 us
    another operation x42, matrix products, spd_solve(): return jax.scipy.linalg.cho_solve((factor, True), rhs_matrix)  31.8 us
  transfers between devices with their start and end apart: 17, of which 15 were waited for; matrix products, arithmetic and copies ran while one was open for 18% of the time, Pallas kernels for 0%

profile of v1, /device:TPU:0, one launch (start us, length us, event | category | flops | bytes accessed | tf_op | source)
XLA Modules:
  0.0 1241.8 jit_solution(13881982140511247523)
XLA Ops:
  9.2 2.9 collective-permute-start
  12.1 3.8 collective-permute-done
  17.9 6.0 collective-permute-done.1
  32.5 4.2 collective-permute-done.2
  52.8 32.8 %collective-permute-done.3 = bf16[8,256,256]{2,1,0:T(8,128)(2,1)} collective-permute-done((bf16[8,256,256]{2,1,0:T(8,128)(2,1)}, bf16[8,256,256]{2,1,0:T(8,128)(2,1)}, u32[]{:S(2)}, u32[]{:S(2)}) %collective-permute-start.3) | collective-permute-done | bytes 1048608 | tf_op jit(solution)/shard_map/ppermute | solution.py:21
  88.9 9.8 while.62
  100.9 8.7 while.60
  112.0 93.5 %reduce-scatter.3.cloned.1.call-done = f32[256,256]{1,0:T(8,128)} async-done(((f32[4096,256]{1,0:T(8,128)}), f32[256,256]{1,0:T(8,128)}) %reduce-scatter.3.cloned.1.call-update) | async-done | bytes 262160 | tf_op jit(solution)/shard_map/reduce_scatter | solution.py:102
  208.0 114.9 %all-reduce.10.cloned.1.call-done = (f32[1,512,256]{1,2,0:T(8,128)}, f32[1,512,256]{1,2,0:T(8,128)}) async-done(((f32[1,512,256]{1,2,0:T(8,128)}, f32[1,512,256]{1,2,0:T(8,128)}), (f32[1,512,256]{1,2,0:T(8,128)}, f32[1,512,256]{1,2,0:T(8,128)})) %all-reduce.10.cloned.1.call-update) | async-done | bytes 1048592 | tf_op jit(solution)/shard_map/psum | solution.py:47
  325.3 7.2 all-gather.5.cloned.1.call-done
  337.6 11.7 cholesky.374
  349.5 9.8 custom-call.35
  361.9 11.7 cholesky.393
  373.6 10.0 custom-call.36
  385.2 11.7 cholesky.414
  397.6 9.8 custom-call.37
  408.8 11.7 cholesky.431
  426.0 11.5 while.64
  437.5 39.3 %custom-call.38 = f32[4,128,128]{1,2,0:T(8,128)S(1)} custom-call(f32[4,128,128]{2,1,0:T(8,128)S(1)} %get-tuple-element.377), custom_call_target="InvertDiagBlocksLowerTriangular" | custom-call | tf_op jit(solution)/shard_map/jit(_cho_solve)/triangular_solve | solution.py:36
  491.9 11.7 cholesky.446
  504.4 10.8 custom-call.39
  519.1 12.5 %cholesky.465 = f32[128,128]{1,0:T(8,128)S(1)} custom-call(f32[128,128]{1,0:T(8,128)} %cholesky.603), custom_call_target="Cholesky" | custom-call | tf_op jit(solution)/shard_map/jit(cholesky)/cholesky | solution.py:35
  532.3 10.6 custom-call.40
  546.1 12.5 %cholesky.486 = f32[128,128]{1,0:T(8,128)} custom-call(f32[128,128]{1,0:T(8,128)S(1)} %cholesky.608), custom_call_target="Cholesky" | custom-call | tf_op jit(solution)/shard_map/jit(cholesky)/cholesky | solution.py:35
  560.1 10.4 custom-call.41
  572.9 12.3 cholesky.503
  595.4 105.3 %all-reduce.6.cloned.1.call-done = f32[1,512,256]{2,1,0:T(8,128)} async-done(((f32[1,512,256]{2,1,0:T(8,128)}), f32[1,512,256]{2,1,0:T(8,128)}) %all-reduce.6.cloned.1.call-update) | async-done | bytes 524304 | tf_op jit(solution)/shard_map/psum | solution.py:47
  701.5 14.3 %while.65 = (s32[]{:T(128)}, f32[512,512]{1,0:T(8,128)}, s32[4,2]{0,1:T(2,128)S(1)}, f32[4,128,128]{2,1,0:T(8,128)}, s32[]{:T(128)}) while((s32[]{:T(128)}, f32[512,512]{1,0:T(8,128)}, s32[4,2]{0,1:T(2,128)S(1)}, f32[4,128,128]{2,1,0:T(8,128)}, s32[]{:T(128)}) %tuple.233), condition=%wide.while_cond.clone, body=%wide.while_body.clone.sunk | while | flops 2 | bytes 132705 | solution.py:36
  709.5 2.9 bitcast_dynamic-update-slice_fusion.7
  715.8 40.8 %custom-call.42 = f32[4,128,128]{1,2,0:T(8,128)} custom-call(f32[4,128,128]{2,1,0:T(8,128)} %get-tuple-element.378), custom_call_target="InvertDiagBlocksLowerTriangular" | custom-call | tf_op jit(solution)/shard_map/jit(_cho_solve)/triangular_solve | solution.py:36
  770.3 3.5 collective-permute-done.4
  775.5 4.9 collective-permute-done.5
  781.3 8.6 collective-permute-done.6
  794.4 40.6 %collective-permute-done.7 = bf16[8,256,256]{2,1,0:T(8,128)(2,1)} collective-permute-done((bf16[8,256,256]{2,1,0:T(8,128)(2,1)}, bf16[8,256,256]{2,1,0:T(8,128)(2,1)}, u32[]{:S(2)}, u32[]{:S(2)}) %collective-permute-start.7) | collective-permute-done | bytes 1048608 | tf_op jit(solution)/shard_map/ppermute | solution.py:21
  838.2 9.8 while.63
  850.2 8.7 while.61
  859.0 94.5 %reduce-scatter.5.cloned.1.call-done = f32[256,256]{1,0:T(8,128)} async-done(((f32[4096,256]{1,0:T(8,128)}), f32[256,256]{1,0:T(8,128)}) %reduce-scatter.5.cloned.1.call-update) | async-done | bytes 262160 | tf_op jit(solution)/shard_map/reduce_scatter | solution.py:102
  956.2 111.1 %all-reduce.8.cloned.1.call-done = f32[1,512,256]{1,2,0:T(8,128)} async-done(((f32[1,512,256]{1,2,0:T(8,128)}), f32[1,512,256]{1,2,0:T(8,128)}) %all-reduce.8.cloned.1.call-update) | async-done | bytes 524304 | tf_op jit(solution)/shard_map/psum | solution.py:47
  1068.4 8.5 all-gather.11.cloned.1.call-done
  1082.0 11.7 cholesky.518
  1093.9 9.8 custom-call.43
  1106.2 11.7 cholesky.537
  1119.3 10.0 custom-call.44
  1130.9 11.7 cholesky.558
  1143.3 9.8 custom-call.45
  1154.6 11.7 cholesky.575
  1170.9 11.7 while.66
  1182.6 39.3 %custom-call.46 = f32[4,128,128]{1,2,0:T(8,128)S(1)} custom-call(f32[4,128,128]{2,1,0:T(8,128)S(1)} %get-tuple-element.379), custom_call_target="InvertDiagBlocksLowerTriangular" | custom-call | tf_op jit(solution)/shard_map/jit(_cho_solve)/triangular_solve | solution.py:36
  (312 shorter events, 219.8 us)
Async XLA Ops:
  6.5 19.1 %copy-start = (bf16[192,128]{1,0:T(8,128)(2,1)S(1)}, bf16[192,128]{1,0:T(8,128)(2,1)}, u32[]{:S(2)}) copy-start(bf16[192,128]{1,0:T(8,128)(2,1)} %param.15) | copy-start | bytes 147460
  6.5 11.3 copy-start.31
  6.5 199.0 %reduce-scatter.3.cloned.1.call-start = ((), (), s32[]{:S(2)}) async-start(), calls=%async_computation.2 | async-start | bytes 4456448 | tf_op jit(solution)/shard_map/reduce_scatter | solution.py:102
  9.2 6.7 collective-permute-start
  16.0 7.8 collective-permute-start.1
  23.9 1.7 copy-start.21
  23.9 1.7 copy-start.22
  24.0 12.7 %collective-permute-start.2 = (bf16[4,256,256]{2,1,0:T(8,128)(2,1)S(1)}, bf16[4,256,256]{2,1,0:T(8,128)(2,1)}, u32[]{:S(2)}, u32[]{:S(2)}) collective-permute-start(bf16[4,256,256]{2,1,0:T(8,128)(2,1)S(1)} %pad_maximum_fusion.5), channel_id=1, source_target_pairs={{0,8},{2,10},{4,12},{6,14},{8,0},{10,2},{12,4},{14,6},{16,24},{18,... | collective-permute-start | bytes 1572872 | tf_op jit(solution)/shard_map/ppermute | solution.py:21
  39.0 46.6 %collective-permute-start.3 = (bf16[8,256,256]{2,1,0:T(8,128)(2,1)}, bf16[8,256,256]{2,1,0:T(8,128)(2,1)}, u32[]{:S(2)}, u32[]{:S(2)}) collective-permute-start(bf16[8,256,256]{2,1,0:T(8,128)(2,1)} %pad_maximum_fusion.2), channel_id=1, source_target_pairs={{0,16},{2,18},{4,20},{6,22},{8,24},{10,26},{12,28},{14,30},{16,0},... | collective-permute-start | bytes 3145736 | tf_op jit(solution)/shard_map/ppermute | solution.py:21
  109.6 0.9 copy-start.24
  109.6 213.3 %all-reduce.10.cloned.1.call-start = ((), (), s32[]{:S(2)}) async-start(), calls=%async_computation.10 | async-start | bytes 2097152 | tf_op jit(solution)/shard_map/psum | solution.py:47
  207.9 124.6 %all-gather.5.cloned.1.call-start = ((), (), s32[]{:S(2)}) async-start(), calls=%async_computation.3 | async-start | bytes 1572864 | tf_op jit(solution)/shard_map/all_gather | solution.py:48
  322.9 154.0 %all-gather.7.cloned.1.call-start = ((), (), s32[]{:S(2)}) async-start(), calls=%async_computation.4 | async-start | bytes 1572864 | tf_op jit(solution)/shard_map/all_gather | solution.py:48
  325.3 375.4 %all-reduce.6.cloned.1.call-start = ((), (), s32[]{:S(2)}) async-start(), calls=%async_computation.5 | async-start | bytes 1048576 | tf_op jit(solution)/shard_map/psum | solution.py:47
  332.6 2.6 copy-start.12
  336.6 1.0 copy-start.18
  476.8 7.9 copy-start.25
  476.9 2.6 copy-start.2
  479.5 2.3 copy-start.10
  485.1 3.4 copy-start.26
  488.1 1.5 copy-start.3
  488.6 2.2 copy-start.13
  488.9 2.0 copy-start.15
  491.0 1.0 copy-start.19
  517.7 0.7 copy-start.28
  585.2 7.7 copy-start.30
  587.6 0.8 copy-start.5
  590.2 166.4 %all-gather.9.cloned.1.call-start = ((), (), s32[]{:S(2)}) async-start(), calls=%async_computation.6 | async-start | bytes 1572864 | tf_op jit(solution)/shard_map/all_gather | solution.py:48
  700.7 252.8 %reduce-scatter.5.cloned.1.call-start = ((), (), s32[]{:S(2)}) async-start(), calls=%async_computation.7 | async-start | bytes 4456448 | tf_op jit(solution)/shard_map/reduce_scatter | solution.py:102
  715.8 44.9 %copy-start.9 = (f32[512,512]{1,0:T(8,128)S(1)}, f32[512,512]{1,0:T(8,128)}, u32[]{:S(2)}) copy-start(f32[512,512]{1,0:T(8,128)} %get-tuple-element.856) | copy-start | bytes 3145732
  756.7 5.5 copy-start.27
  766.2 1.4 copy-start.6
  768.8 5.0 collective-permute-start.4
  773.9 6.4 collective-permute-start.5
  780.5 9.4 collective-permute-start.6
  790.0 0.8 copy-start.7
  790.0 1.9 copy-start.8
  791.9 43.1 %collective-permute-start.7 = (bf16[8,256,256]{2,1,0:T(8,128)(2,1)}, bf16[8,256,256]{2,1,0:T(8,128)(2,1)}, u32[]{:S(2)}, u32[]{:S(2)}) collective-permute-start(bf16[8,256,256]{2,1,0:T(8,128)(2,1)} %pad_maximum_fusion.4), channel_id=1, source_target_pairs={{0,16},{2,18},{4,20},{6,22},{8,24},{10,26},{12,28},{14,30},{16,0},... | collective-permute-start | bytes 3145736 | tf_op jit(solution)/shard_map/ppermute | solution.py:21
  858.9 208.4 %copy-start.4 = (f32[128,512]{1,0:T(8,128)S(1)}, f32[128,512]{1,0:T(8,128)}, u32[]{:S(2)}) copy-start(f32[128,512]{1,0:T(8,128)} %copy-done.3) | copy-start | bytes 786436
  858.9 208.4 %copy-start.16 = (f32[128,512]{1,0:T(8,128)S(1)}, f32[128,512]{1,0:T(8,128)}, u32[]{:S(2)}) copy-start(f32[128,512]{1,0:T(8,128)} %copy-done.15) | copy-start | bytes 786436
  858.9 208.4 %copy-start.23 = (f32[128,512]{1,0:T(8,128)S(1)}, f32[128,512]{1,0:T(8,128)}, u32[]{:S(2)}) copy-start(f32[128,512]{1,0:T(8,128)} %fusion.172) | copy-start | bytes 786436
  859.0 208.4 %all-reduce.8.cloned.1.call-start = ((), (), s32[]{:S(2)}) async-start(), calls=%async_computation.8 | async-start | bytes 1048576 | tf_op jit(solution)/shard_map/psum | solution.py:47
  956.0 120.9 %all-gather.11.cloned.1.call-start = ((), (), s32[]{:S(2)}) async-start(), calls=%async_computation.9 | async-start | bytes 1572864 | tf_op jit(solution)/shard_map/all_gather | solution.py:48
  1076.9 2.6 copy-start.14
  1081.0 1.0 copy-start.17
  1182.6 42.5 %copy-start.11 = (f32[512,512]{1,0:T(8,128)S(1)}, f32[512,512]{1,0:T(8,128)}, u32[]{:S(2)}) copy-start(f32[512,512]{1,0:T(8,128)} %get-tuple-element.858) | copy-start | bytes 3145732
  1231.6 1.4 copy-start.20
  1231.6 3.3 copy-start.1
  (1 other events, 0.7 us)
Sparse Core Ops, SparseCore 0:
  109.7 95.7 reduce-scatter.2
  210.8 111.9 all-reduce.9
  324.4 8.0 all-gather.4
  333.9 10.2 all-gather.6
  590.3 110.3 all-reduce.5
  702.1 8.0 all-gather.8
  859.0 94.4 reduce-scatter.4
  958.7 108.5 all-reduce.7
  1068.9 8.0 all-gather.10
